TPU v7x, 32 devices: a whole 2x2x4 slice. The times are simulated.
32 devices in a mesh: rows: 32 (over z, y, x, core).
Axes of the slice: x: 2, y: 2, z: 4, core: 2. Of those that a mesh axis runs over, the one named last changes fastest.
Arguments:
- band_lower: float32 [512, 128, 128], P('rows'), may hold values from -1.1 to 0.15, as said below
- band_diag: float32 [512, 128, 128], P('rows'), may hold values from -0.3 to 5.3
- band_upper: float32 [512, 128, 128], P('rows'), may hold values from -0.15 to 1.1, as said below
- fac_lower: float32 [512, 128, 128], P('rows'), may hold values from -1 to 0.1
- pivot_inverse: float32 [512, 128, 128], P('rows'), may hold values from -0.08 to 1.08
- rhs: float32 [128, 65536], P(None, 'rows'), may hold values from -150 to 150
- start: float32 [128, 65536], P(None, 'rows'), may hold values from -0.6 to 0.6
Outputs:
- solution: float32 [128, 65536], P(None, 'rows')
- krylov: float32 [4, 128, 65536], P(None, None, 'rows')
- hessenberg: float32 [4, 3, 128], replicated
Inputs may be any that keep to these rules, and one draw needn't show every extreme that they name: `band_lower`: each block is zero below its diagonal, so the band reaches 128 diagonals on each side of the main one. `band_upper`: each block is zero above its diagonal.
All inputs are finite; a program needn't handle non-finite values.
Results may differ from a plain program's by a relative error of at most 0.00024.
Values sent between devices are 32-bit elements; how exact they have to be, the bound alone decides.
A program may use at most 128 MiB of HBM per device.

v0:
```python
import jax
import jax.numpy as jnp
from jax import lax
from jax.sharding import PartitionSpec as P

ITERS = 3


highest = lax.Precision.HIGHEST
epsilon = 1e-06


def padded_2(array, sides, width):
    for axis, dim in sides:
        size, length = (lax.axis_size(axis), array.shape[dim])
        up = [(i, (i + 1) % size) for i in range(size - 1)]
        down = [(j, i) for i, j in up]
        last = lax.slice_in_dim(array, length - width, length, axis=dim)
        first = lax.slice_in_dim(array, 0, width, axis=dim)
        before = lax.ppermute(last, axis, up)
        after = lax.ppermute(first, axis, down)
        array = jnp.concatenate([before, array, after], axis=dim)
    return array


def passed_along(value, axis, steps):
    count = lax.axis_size(axis)
    first, last = (max(0, -steps), min(count, count - steps))
    return lax.ppermute(value, axis, [(source, source + steps) for source in range(first, last)])


def block_apply(matrices, vectors):
    return jnp.einsum("...ij,c...j->c...i", matrices, vectors, precision=highest)


def local_solve(source, fac_lower, pivot_inverse, band_upper):
    length = source.shape[-2]
    forward = [source[..., 0, :]]
    for position in range(1, length):
        forward.append(
            source[..., position, :] - block_apply(fac_lower[..., position, :, :], forward[-1])
        )
    backward = [block_apply(pivot_inverse[..., length - 1, :, :], forward[-1])]
    for position in range(length - 2, -1, -1):
        remainder = forward[position] - block_apply(band_upper[..., position, :, :], backward[-1])
        backward.append(block_apply(pivot_inverse[..., position, :, :], remainder))
    return jnp.stack(backward[::-1], axis=-2)


def least_squares(hessenberg, start_norm):
    columns_total = hessenberg.shape[1]
    matrix = [
        [hessenberg[row_pos, col_pos] for col_pos in range(columns_total)]
        for row_pos in range(columns_total + 1)
    ]
    target = [start_norm] + [jnp.zeros_like(start_norm) for row_pos in range(columns_total)]
    cos_terms = []
    sin_terms = []
    for col_pos in range(columns_total):
        for row_pos in range(col_pos):
            upper_entry = matrix[row_pos][col_pos]
            lower_entry = matrix[row_pos + 1][col_pos]
            matrix[row_pos][col_pos] = (
                cos_terms[row_pos] * upper_entry + sin_terms[row_pos] * lower_entry
            )
            matrix[row_pos + 1][col_pos] = (
                cos_terms[row_pos] * lower_entry - sin_terms[row_pos] * upper_entry
            )
        upper_entry = matrix[col_pos][col_pos]
        lower_entry = matrix[col_pos + 1][col_pos]
        radius = jnp.sqrt(upper_entry * upper_entry + lower_entry * lower_entry)
        cos_terms.append(upper_entry / radius)
        sin_terms.append(lower_entry / radius)
        matrix[col_pos][col_pos] = radius
        target[col_pos + 1] = -sin_terms[col_pos] * target[col_pos]
        target[col_pos] = cos_terms[col_pos] * target[col_pos]
    weights = [None] * columns_total
    for row_pos in range(columns_total - 1, -1, -1):
        partial_sum = target[row_pos]
        for col_pos in range(row_pos + 1, columns_total):
            partial_sum = partial_sum - matrix[row_pos][col_pos] * weights[col_pos]
        weights[row_pos] = partial_sum / matrix[row_pos][row_pos]
    return weights


def invert_coupling(coupling):
    normal_matrix = jnp.dot(coupling.T, coupling, precision=highest)
    factor = jnp.linalg.cholesky(normal_matrix)
    return jax.scipy.linalg.cho_solve((factor, True), coupling.T)


def apply_matrix(field, band_lower, band_diag, band_upper):
    padded = padded_2(field, (("rows", 1),), 1)
    return (
        block_apply(band_diag, field)
        + block_apply(band_lower, padded[:, :-2])
        + block_apply(band_upper, padded[:, 2:])
    )


def local(band_lower, band_diag, band_upper, fac_lower, pivot_inverse, rhs, start):
    blocks = band_diag.shape[0]
    block_width = band_diag.shape[1]
    systems = rhs.shape[0]
    zero_blocks = jnp.zeros((block_width, blocks - 1, block_width), jnp.float32)
    left_source = jnp.concatenate([band_lower[0].T[:, None, :], zero_blocks], axis=1)
    right_source = jnp.concatenate([zero_blocks, band_upper[-1].T[:, None, :]], axis=1)
    left_spike = local_solve(left_source, fac_lower, pivot_inverse, band_upper)
    right_spike = local_solve(right_source, fac_lower, pivot_inverse, band_upper)
    top_tip = left_spike[:, 0, :].T
    bottom_tip = right_spike[:, -1, :].T
    identity = jnp.eye(block_width, dtype=jnp.float32)
    prev_bottom = passed_along(bottom_tip, "rows", 1)
    own_inverse = invert_coupling(identity - jnp.dot(top_tip, prev_bottom, precision=highest))

    def precondition(field):
        solved_local = local_solve(field, fac_lower, pivot_inverse, band_upper)
        top_values = solved_local[:, 0, :]
        bottom_values = solved_local[:, -1, :]
        prev_values = passed_along(bottom_values, "rows", 1)
        top_solved = block_apply(own_inverse, top_values - block_apply(top_tip, prev_values))
        next_solved = passed_along(top_solved, "rows", -1)
        bottom_solved = prev_values - block_apply(prev_bottom, top_solved)
        result = solved_local - jnp.einsum(
            "cki,sc->ski", right_spike, next_solved, precision=highest
        )
        return result - jnp.einsum("cki,sc->ski", left_spike, bottom_solved, precision=highest)

    fields = rhs.reshape(systems, blocks, block_width)
    start_blocks = start.reshape(systems, blocks, block_width)
    residual = fields - apply_matrix(start_blocks, band_lower, band_diag, band_upper)
    start_norm = jnp.sqrt(lax.psum(jnp.sum(residual * residual, axis=(1, 2)), "rows") + epsilon)
    krylov = [residual / start_norm[:, None, None]]
    columns = []
    for column in range(ITERS):
        mapped = apply_matrix(precondition(krylov[column]), band_lower, band_diag, band_upper)
        stacked = jnp.stack(krylov)
        local_products = jnp.einsum("jsbk,sbk->js", stacked, mapped, precision=highest)
        products, squares = lax.psum(
            (local_products, jnp.sum(mapped * mapped, axis=(1, 2))), "rows"
        )
        update = mapped - jnp.einsum("js,jsbk->sbk", products, stacked, precision=highest)
        length_now = jnp.sqrt(
            jnp.maximum(squares - jnp.sum(products * products, axis=0), 0.0) + epsilon
        )
        krylov.append(update / length_now[:, None, None])
        columns.append(
            jnp.concatenate(
                [products, length_now[None], jnp.zeros((ITERS - 1 - column, systems), jnp.float32)],
                axis=0,
            )
        )
    hessenberg = jnp.stack(columns, axis=1)
    weights = least_squares(hessenberg, start_norm)
    combined = weights[0][:, None, None] * krylov[0]
    for column in range(1, ITERS):
        combined = combined + weights[column][:, None, None] * krylov[column]
    solution = start_blocks + precondition(combined)
    return (
        solution.reshape(systems, -1),
        jnp.stack(krylov).reshape(ITERS + 1, systems, -1),
        hessenberg,
    )


def solution(mesh):
    return jax.shard_map(
        local,
        mesh=mesh,
        in_specs=(
            P("rows", None, None),
            P("rows", None, None),
            P("rows", None, None),
            P("rows", None, None),
            P("rows", None, None),
            P(None, "rows"),
            P(None, "rows"),
        ),
        out_specs=(P(None, "rows"), P(None, None, "rows"), P()),
        check_vma=False,
    )
```

profile of v0, /device:TPU:0, one launch (start us, length us, event | category | flops | bytes accessed | tf_op | source)
XLA Modules:
  0.0 515.4 jit_solution(4449329403102840863)
XLA Ops:
  0.6 2.6 copy.93
  3.3 2.7 copy.96
  7.0 3.0 collective-permute-start
  24.8 4.9 collective-permute-start.3
  59.3 13.2 %constant_dynamic-update-slice_fusion.23 = f32[128,16,128]{2,0,1:T(8,128)} fusion(f32[128,16,128]{2,0,1:T(8,128)} %constant_dynamic-update-slice_fusion.24, f32[128,128]{1,0:T(8,128)S(1)} %fusion.197), kind=kLoop, calls=%fused_computation.279 | loop fusion | bytes 131072
  79.5 2.6 copy.159
  82.0 2.6 copy.157
  85.3 4.3 convolution_add_fusion.7
  89.6 4.1 multiply_reduce_fusion.6
  93.8 41.9 %psum.49 = f32[128]{0:T(128)S(1)} all-reduce(f32[128]{0:T(128)S(1)} %get-tuple-element.29), channel_id=1, replica_groups=mesh['rows'=32] {'rows'}, use_global_device_ids=true, to_apply=%region_1.2 | all-reduce | flops 128 | bytes 1024 | tf_op jit(solution)/shard_map/psum | solution.py:132
  155.8 13.2 %cholesky.16 = f32[128,128]{1,0:T(8,128)} custom-call(f32[128,128]{1,0:T(8,128)} %fusion.46), custom_call_target="Cholesky" | custom-call | tf_op jit(solution)/shard_map/jit(cholesky)/cholesky | solution.py:88
  172.7 11.3 %custom-call.10 = f32[1,128,128]{1,2,0:T(8,128)} custom-call(f32[1,128,128]{2,1,0:T(8,128)} %fusion.38), custom_call_target="InvertDiagBlocksLowerTriangular" | custom-call | tf_op jit(solution)/shard_map/jit(_cho_solve)/triangular_solve | solution.py:89
  217.4 5.0 collective-permute-start.5
  228.9 3.3 multiply_reduce_fusion.2
  232.2 43.5 %all-reduce.2 = (f32[128]{0:T(128)S(1)}, f32[1,128]{1,0:T(1,128)S(1)}) all-reduce(f32[128]{0:T(128)S(1)} %get-tuple-element.7, f32[1,128]{1,0:T(1,128)S(1)} %bitcast.1614), channel_id=1, replica_groups=mesh['rows'=32] {'rows'}, use_global_device_ids=true, to_apply=%region_7.8 | all-reduce | flops 256 | bytes 2048 | tf_op jit(solution)/shard_map/psum | solution.py:139
  314.9 2.6 fusion.3
  317.5 5.0 collective-permute-start.9
  332.2 42.5 %all-reduce.1 = (f32[2,128]{1,0:T(2,128)S(1)}, f32[128]{0:T(128)S(1)}) all-reduce(f32[2,128]{1,0:T(2,128)S(1)} %bitcast.1613, f32[128]{0:T(128)S(1)} %get-tuple-element.38), channel_id=1, replica_groups=mesh['rows'=32] {'rows'}, use_global_device_ids=true, to_apply=%region_8.9 | all-reduce | flops 384 | bytes 3072 | tf_op jit(solution)/shard_map/psum | solution.py:139
  404.2 2.6 copy.162
  412.9 2.6 fusion.2
  415.6 5.0 collective-permute-start.13
  430.2 42.9 %all-reduce = (f32[128]{0:T(128)S(1)}, f32[3,128]{1,0:T(4,128)S(1)}) all-reduce(f32[128]{0:T(128)S(1)} %get-tuple-element.42, f32[3,128]{1,0:T(4,128)S(1)} %bitcast.1608), channel_id=1, replica_groups=mesh['rows'=32] {'rows'}, use_global_device_ids=true, to_apply=%region_14.15 | all-reduce | flops 512 | bytes 4096 | tf_op jit(solution)/shard_map/psum | solution.py:139
  500.0 4.5 pad_maximum_fusion
  508.5 2.8 collective-permute-done.16
  (597 shorter events, 243.0 us)
Async XLA Ops:
  0.6 29.4 %copy-start = (f32[16,128,128]{2,1,0:T(8,128)S(1)}, f32[16,128,128]{2,1,0:T(8,128)}, u32[]{:S(2)}) copy-start(f32[16,128,128]{2,1,0:T(8,128)} %param.8) | copy-start | bytes 3145732
  6.0 24.0 %copy-start.21 = (f32[128,2048]{0,1:T(8,128)S(1)}, f32[128,2048]{0,1:T(8,128)}, u32[]{:S(2)}) copy-start(f32[128,2048]{0,1:T(8,128)} %copy.93) | copy-start | bytes 3145732
  7.0 78.3 %collective-permute-start = (f32[128,1,128]{2,0,1:T(8,128)S(1)}, f32[128,1,128]{2,0,1:T(8,128)}, u32[]{:S(2)}, u32[]{:S(2)}) collective-permute-start(f32[128,1,128]{2,0,1:T(8,128)S(1)} %get-tuple-element.28), channel_id=1, source_target_pairs={{0,1},{1,2},{2,3},{3,4},{4,5},{5,6},{6,7},{7,8},{8,9},{9,10},{10,1... | collective-permute-start | bytes 196616 | tf_op jit(solution)/shard_map/ppermute | solution.py:20
  10.0 79.6 %collective-permute-start.1 = (f32[128,1,128]{2,0,1:T(8,128)S(1)}, f32[128,1,128]{2,0,1:T(8,128)}, u32[]{:S(2)}, u32[]{:S(2)}) collective-permute-start(f32[128,1,128]{2,0,1:T(8,128)S(1)} %get-tuple-element.27), channel_id=1, source_target_pairs={{1,0},{2,1},{3,2},{4,3},{5,4},{6,5},{7,6},{8,7},{9,8},{10,9},{11,1... | collective-permute-start | bytes 196616 | tf_op jit(solution)/shard_map/ppermute | solution.py:21
  24.8 128.2 %collective-permute-start.3 = (f32[128,128]{0,1:T(8,128)S(1)}, f32[128,128]{0,1:T(8,128)S(1)}, u32[]{:S(2)}, u32[]{:S(2)}) collective-permute-start(f32[128,128]{0,1:T(8,128)S(1)} %bitcast.1605), channel_id=1, source_target_pairs={{0,1},{1,2},{2,3},{3,4},{4,5},{5,6},{6,7},{7,8},{8,9},{9,10},{10,1... | collective-permute-start | bytes 196616 | tf_op jit(solution)/shard_map/ppermute | solution.py:29
  140.7 67.9 %collective-permute-start.2 = (f32[128,128]{1,0:T(8,128)S(1)}, f32[128,128]{1,0:T(8,128)}, u32[]{:S(2)}, u32[]{:S(2)}) collective-permute-start(f32[128,128]{1,0:T(8,128)S(1)} %fusion.327), channel_id=1, source_target_pairs={{0,1},{1,2},{2,3},{3,4},{4,5},{5,6},{6,7},{7,8},{8,9},{9,10},{10,1... | collective-permute-start | bytes 196616 | tf_op jit(solution)/shard_map/ppermute | solution.py:29
  155.8 48.3 %copy-start.39 = (f32[128,128]{1,0:T(8,128)S(1)}, f32[128,128]{1,0:T(8,128)}, u32[]{:S(2)}) copy-start(f32[128,128]{1,0:T(8,128)} %copy-done.38) | copy-start | bytes 196612
  210.0 5.0 collective-permute-start.4
  217.4 8.7 %collective-permute-start.5 = (f32[128,1,128]{2,0,1:T(8,128)S(1)}, f32[128,1,128]{2,0,1:T(8,128)S(1)}, u32[]{:S(2)}, u32[]{:S(2)}) collective-permute-start(f32[128,1,128]{2,0,1:T(8,128)S(1)} %get-tuple-element.26), channel_id=1, source_target_pairs={{0,1},{1,2},{2,3},{3,4},{4,5},{5,6},{6,7},{7,8},{8,9},{9,10},{10,1... | collective-permute-start | bytes 196616 | tf_op jit(solution)/shard_map/ppermute | solution.py:20
  224.7 4.2 collective-permute-start.6
  275.6 29.6 %copy-start.55 = (f32[128]{0:T(128)}, f32[128]{0:T(128)S(1)}, u32[]{:S(2)}) copy-start(f32[128]{0:T(128)S(1)} %fusion.710) | copy-start | bytes 1540
  285.3 23.5 %collective-permute-start.7 = (f32[128,128]{1,0:T(8,128)S(1)}, f32[128,128]{1,0:T(8,128)S(1)}, u32[]{:S(2)}, u32[]{:S(2)}) collective-permute-start(f32[128,128]{1,0:T(8,128)S(1)} %fusion.321), channel_id=1, source_target_pairs={{0,1},{1,2},{2,3},{3,4},{4,5},{5,6},{6,7},{7,8},{8,9},{9,10},{10,1... | collective-permute-start | bytes 196616 | tf_op jit(solution)/shard_map/ppermute | solution.py:29
  309.2 5.7 %collective-permute-start.8 = (f32[128,128]{1,0:T(8,128)S(1)}, f32[128,128]{1,0:T(8,128)S(1)}, u32[]{:S(2)}, u32[]{:S(2)}) collective-permute-start(f32[128,128]{1,0:T(8,128)S(1)} %fusion.735), channel_id=1, source_target_pairs={{1,0},{2,1},{3,2},{4,3},{5,4},{6,5},{7,6},{8,7},{9,8},{10,9},{11,1... | collective-permute-start | bytes 196616 | tf_op jit(solution)/shard_map/ppermute | solution.py:29
  317.5 8.9 %collective-permute-start.9 = (f32[128,1,128]{2,0,1:T(8,128)S(1)}, f32[128,1,128]{2,0,1:T(8,128)S(1)}, u32[]{:S(2)}, u32[]{:S(2)}) collective-permute-start(f32[128,1,128]{2,0,1:T(8,128)S(1)} %get-tuple-element.24), channel_id=1, source_target_pairs={{0,1},{1,2},{2,3},{3,4},{4,5},{5,6},{6,7},{7,8},{8,9},{9,10},{10,1... | collective-permute-start | bytes 196616 | tf_op jit(solution)/shard_map/ppermute | solution.py:20
  324.8 4.0 collective-permute-start.10
  376.7 24.9 %copy-start.61 = (f32[128]{0:T(128)}, f32[128]{0:T(128)S(1)}, u32[]{:S(2)}) copy-start(f32[128]{0:T(128)S(1)} %add_sqrt_fusion.2) | copy-start | bytes 1540
  377.9 24.4 %copy-start.2 = (f32[128,16,128]{0,2,1:T(8,128)}, f32[128,16,128]{0,2,1:T(8,128)S(1)}, u32[]{:S(2)}) copy-start(f32[128,16,128]{0,2,1:T(8,128)S(1)} %subtract_divide_fusion.1) | copy-start | bytes 3145732
  381.4 25.4 %collective-permute-start.11 = (f32[128,128]{1,0:T(8,128)S(1)}, f32[128,128]{1,0:T(8,128)S(1)}, u32[]{:S(2)}, u32[]{:S(2)}) collective-permute-start(f32[128,128]{1,0:T(8,128)S(1)} %fusion.319), channel_id=1, source_target_pairs={{0,1},{1,2},{2,3},{3,4},{4,5},{5,6},{6,7},{7,8},{8,9},{9,10},{10,1... | collective-permute-start | bytes 196616 | tf_op jit(solution)/shard_map/ppermute | solution.py:29
  407.3 5.6 %collective-permute-start.12 = (f32[128,128]{1,0:T(8,128)S(1)}, f32[128,128]{1,0:T(8,128)S(1)}, u32[]{:S(2)}, u32[]{:S(2)}) collective-permute-start(f32[128,128]{1,0:T(8,128)S(1)} %fusion.738), channel_id=1, source_target_pairs={{1,0},{2,1},{3,2},{4,3},{5,4},{6,5},{7,6},{8,7},{9,8},{10,9},{11,1... | collective-permute-start | bytes 196616 | tf_op jit(solution)/shard_map/ppermute | solution.py:29
  415.6 8.9 %collective-permute-start.13 = (f32[128,1,128]{2,0,1:T(8,128)S(1)}, f32[128,1,128]{2,0,1:T(8,128)S(1)}, u32[]{:S(2)}, u32[]{:S(2)}) collective-permute-start(f32[128,1,128]{2,0,1:T(8,128)S(1)} %get-tuple-element.22), channel_id=1, source_target_pairs={{0,1},{1,2},{2,3},{3,4},{4,5},{5,6},{6,7},{7,8},{8,9},{9,10},{10,1... | collective-permute-start | bytes 196616 | tf_op jit(solution)/shard_map/ppermute | solution.py:20
  422.9 4.0 collective-permute-start.14
  429.2 43.9 %copy-start.56 = (f32[128]{0:T(128)S(1)}, f32[128]{0:T(128)}, u32[]{:S(2)}) copy-start(f32[128]{0:T(128)} %copy-done.55) | copy-start | bytes 1540
  480.9 24.2 %collective-permute-start.15 = (f32[128,128]{0,1:T(8,128)S(1)}, f32[128,128]{0,1:T(8,128)S(1)}, u32[]{:S(2)}, u32[]{:S(2)}) collective-permute-start(f32[128,128]{0,1:T(8,128)S(1)} %fusion.317), channel_id=1, source_target_pairs={{0,1},{1,2},{2,3},{3,4},{4,5},{5,6},{6,7},{7,8},{8,9},{9,10},{10,1... | collective-permute-start | bytes 196616 | tf_op jit(solution)/shard_map/ppermute | solution.py:29
  505.7 5.7 %collective-permute-start.16 = (f32[128,128]{1,0:T(8,128)S(1)}, f32[128,128]{1,0:T(8,128)S(1)}, u32[]{:S(2)}, u32[]{:S(2)}) collective-permute-start(f32[128,128]{1,0:T(8,128)S(1)} %fusion.741), channel_id=1, source_target_pairs={{1,0},{2,1},{3,2},{4,3},{5,4},{6,5},{7,6},{8,7},{9,8},{10,9},{11,1... | collective-permute-start | bytes 196616 | tf_op jit(solution)/shard_map/ppermute | solution.py:29
  (59 other events, 355.5 us)
where the time goes:
time: 524 us; the launch traced here: 515 us
  blocking collectives  171 us (33%)
  matrix products  142 us (27%)
  local copies, waits for them, and re-layouts  97.1 us (19%)
  other arithmetic  53.4 us (10%)
  starting transfers between devices  40.6 us (8%)
  waiting for transfers between devices  7.57 us (1%)
    psum x3, blocking collectives, local(): lax.psum((local_products, jnp.sum(mapped * mapped, axis=(1, 2))), 'rows')  129 us
    dot_general x299, matrix products, block_apply(): jnp.einsum('...ij,c...j->c...i', matrices, vectors, precision=highest)  123 us
    unnamed x219, local copies, waits for them, and re-layouts  75.9 us
    psum x1, blocking collectives, local(): lax.psum(jnp.sum(residual * residual, axis=(1, 2)), 'rows') + epsilon  41.9 us
    ppermute x4, starting transfers between devices, padded_2(): before = lax.ppermute(last, axis, up)  18 us
    ppermute x9, starting transfers between devices, passed_along(): lax.ppermute(value, axis, [(source, source + steps) for source in range(f...  16.7 us
    another operation x3, other arithmetic, invert_coupling(): factor = jnp.linalg.cholesky(normal_matrix)  14.7 us
    another operation x2, other arithmetic, invert_coupling(): return jax.scipy.linalg.cho_solve((factor, True), coupling.T)  13.4 us
  transfers between devices with their start and end apart: 17, of which 5 were waited for; matrix products, arithmetic and copies ran while one was open for 46% of the time, Pallas kernels for 0%

commit v1 on v0

v1 whole, which is shorter than its diff:
```python
import jax
import jax.numpy as jnp
from jax import lax
from jax.experimental import pallas as pl
from jax.experimental.pallas import tpu as pltpu
from jax.sharding import PartitionSpec as P

ITERS = 3
EPS = 1e-06
F32, BF16 = jnp.float32, jnp.bfloat16
HIGHEST = lax.Precision.HIGHEST


def split(x):
    hi = x.astype(BF16)
    return hi, (x - hi.astype(F32)).astype(BF16)


def row(mt):
    return jnp.concatenate(split(mt), axis=1)


def mm(parts, g):
    halves = [split(part) for part in parts]
    lhs = jnp.concatenate([h for h, _ in halves] + [l for _, l in halves], axis=1)
    out = jnp.dot(lhs, jnp.concatenate([g, g], axis=0), preferred_element_type=F32)
    width = out.shape[1] // 2
    return out[:, :width] + out[:, width:]


def local_solve(f_ref, g_ref, gl, ge, gp, n, b):
    z = f_ref[:, 0:b]
    for k in range(n):
        if k:
            z = f_ref[:, k * b : (k + 1) * b] - mm([z], gl[k])
        g_ref[:, k * b : (k + 1) * b] = mm([z], gp[k])
    y = g_ref[:, (n - 1) * b : n * b]
    for k in range(n - 2, -1, -1):
        y = g_ref[:, k * b : (k + 1) * b] - mm([y], ge[k])
        g_ref[:, k * b : (k + 1) * b] = y


def apply_matrix(p_ref, before, after, ga, phi, plo, n, b, out):
    phi[:, 0:b], plo[:, 0:b] = split(before)
    phi[:, (n + 1) * b :], plo[:, (n + 1) * b :] = split(after)
    for k in range(n):
        hi, lo = split(p_ref[:, k * b : (k + 1) * b])
        phi[:, (k + 1) * b : (k + 2) * b] = hi
        plo[:, (k + 1) * b : (k + 2) * b] = lo
    for k in range(n):
        window = slice(k * b, (k + 3) * b)
        lhs = jnp.concatenate([phi[:, window], plo[:, window]], axis=1)
        g = ga[k]
        res = jnp.dot(lhs, jnp.concatenate([g, g], axis=0), preferred_element_type=F32)
        out(k, res[:, :b] + res[:, b:])


def setup_kernel(bl, bd, bu, fl, pi, gl, ge, gp, ga, gvw, wt, vb, ts):
    n, b = bd.shape[0], bd.shape[1]
    for k in range(n):
        gl[k] = row(fl[k].T)
        pr = row(pi[k].T)
        gp[k] = pr
        ut = bu[k].T
        ga[k, 0:b] = row(bl[k].T)
        ga[k, b : 2 * b] = row(bd[k].T)
        ga[k, 2 * b :] = row(ut)
        ge[k] = row(mm([ut], pr))
    z = bl[0].T
    v = mm([bu[n - 1].T], gp[n - 1])
    vb[...] = v
    gvw[n - 1, 0:b] = row(v)
    for k in range(n):
        if k:
            z = -mm([z], gl[k])
            v = -mm([v], ge[n - 1 - k])
            gvw[n - 1 - k, 0:b] = row(v)
        ts[k] = mm([z], gp[k])
    w = ts[n - 1]
    gvw[n - 1, b:] = row(w)
    for k in range(n - 2, -1, -1):
        w = ts[k] - mm([w], ge[k])
        gvw[k, b:] = row(w)
    wt[...] = w


def inverse_kernel(wt, vbp, x, a):
    b = wt.shape[0]
    eye = (
        lax.broadcasted_iota(jnp.int32, (b, b), 0) == lax.broadcasted_iota(jnp.int32, (b, b), 1)
    ).astype(F32)
    dot = lambda l, r: jnp.dot(l, r, precision=HIGHEST, preferred_element_type=F32)
    t = dot(vbp[...], wt[...])
    a[...] = eye - t
    near = jnp.sum(t * t) < 0.25
    s = a[...]
    x[...] = jnp.where(near, eye + t, s.T / jnp.sum(s * s))

    def body(carry):
        step, _ = carry
        r = eye - dot(a[...], x[...])
        x[...] = x[...] + dot(x[...], r)
        return step + 1, jnp.sum(r * r)

    lax.while_loop(lambda c: (c[0] < 80) & (c[1] > 1e-8), body, (0, jnp.float32(1.0)))


def columns_to_rows(cols):
    m = cols[0].shape[0]
    lane = lax.broadcasted_iota(jnp.int32, (m, m), 1)
    grid = jnp.zeros((m, m), F32)
    for i, col in enumerate(cols):
        grid = jnp.where(lane == i, col, grid)
    return grid.T[0:8]


def rows_to_columns(rows, count):
    m = rows.shape[1]
    grid = jnp.concatenate([rows, jnp.zeros((m - rows.shape[0], m), F32)], axis=0).T
    return [grid[:, i : i + 1] for i in range(count)]


def first_kernel(rhs, start, before, after, ga, gl, ge, gp, r, g, phi, plo):
    n, b = ga.shape[0], before.shape[1]

    def out(k, value):
        r[:, k * b : (k + 1) * b] = rhs[:, k * b : (k + 1) * b] - value

    apply_matrix(start, before[...], after[...], ga, phi, plo, n, b, out)
    local_solve(r, g, gl, ge, gp, n, b)


def pre_kernel(g, gbp, gtn, wt, vbp, sinv, wtn, sinvn, gvw, p):
    n, b = gvw.shape[0], gvw.shape[1] // 2
    xt = mm([g[:, 0:b] - mm([gbp[...]], row(wt[...]))], row(sinv[...]))
    xtn = mm([gtn[...] - mm([g[:, (n - 1) * b :]], row(wtn[...]))], row(sinvn[...]))
    xb = gbp[...] - mm([xt], row(vbp[...]))
    for k in range(n):
        p[:, k * b : (k + 1) * b] = g[:, k * b : (k + 1) * b] - mm([xtn, xb], gvw[k])


def mapped_kernel(j, *refs):
    p, before, after, ga = refs[:4]
    ks = refs[4 : 5 + j]
    w, prods, phi, plo = refs[5 + j :]
    n, b = ga.shape[0], before.shape[1]
    acc = [None] * (j + 2 + (j == 0))

    def out(k, value):
        w[:, k * b : (k + 1) * b] = value
        vs = [kk[:, k * b : (k + 1) * b] for kk in ks]
        terms = [value * v for v in vs] + [value * value]
        if j == 0:
            terms.append(vs[0] * vs[0])
        for i, t in enumerate(terms):
            acc[i] = t if acc[i] is None else acc[i] + t

    apply_matrix(p, before[...], after[...], ga, phi, plo, n, b, out)
    prods[...] = columns_to_rows([jnp.sum(a, axis=1, keepdims=True) for a in acc])


def scalars(j, sums, norm):
    rows = [sums[i : i + 1] for i in range(j + 2)]
    rows[0] = rows[0] / norm
    if j == 0:
        rows = [rows[0] / norm, rows[1] / norm / norm]
    h = rows[: j + 1]
    square = rows[j + 1]
    for x in h:
        square = square - x * x
    return h, jnp.sqrt(jnp.maximum(square, 0.0) + EPS)


def norm_of(sums):
    return jnp.sqrt(sums[2:3] + EPS)


def stack8(rows):
    m = rows[0].shape[1]
    return jnp.concatenate(rows + [jnp.zeros((8 - len(rows), m), F32)], axis=0)


def orth_kernel(j, *refs):
    first, sums, w = refs[:3]
    ks = refs[3 : 4 + j]
    gl, ge, gp, v, g = refs[4 + j : 9 + j]
    n, b = gl.shape[0], gl.shape[1]
    norm = norm_of(first[...])
    h, length = scalars(j, sums[...], norm)
    rows = [x / length for x in h] + [1.0 / length]
    rows[0] = rows[0] / norm
    if j == 0:
        rows[1] = rows[1] / norm
    cols = rows_to_columns(stack8(rows), j + 2)
    for k in range(n):
        s = slice(k * b, (k + 1) * b)
        value = w[:, s] * cols[j + 1]
        for i in range(j + 1):
            value = value - cols[i] * ks[i][:, s]
        v[:, s] = value
    local_solve(v, g, gl, ge, gp, n, b)


def least_squares(matrix, start_norm):
    total = ITERS
    target = [start_norm] + [jnp.zeros_like(start_norm) for _ in range(total)]
    cos_terms, sin_terms = [], []
    for c in range(total):
        for r in range(c):
            up, low = matrix[r][c], matrix[r + 1][c]
            matrix[r][c] = cos_terms[r] * up + sin_terms[r] * low
            matrix[r + 1][c] = cos_terms[r] * low - sin_terms[r] * up
        up, low = matrix[c][c], matrix[c + 1][c]
        radius = jnp.sqrt(up * up + low * low)
        cos_terms.append(up / radius)
        sin_terms.append(low / radius)
        matrix[c][c] = radius
        target[c + 1] = -sin_terms[c] * target[c]
        target[c] = cos_terms[c] * target[c]
    weights = [None] * total
    for r in range(total - 1, -1, -1):
        part = target[r]
        for c in range(r + 1, total):
            part = part - matrix[r][c] * weights[c]
        weights[r] = part / matrix[r][r]
    return weights


def final_kernel(s0, s1, s2, r, k1, k2, w, p0, p1, p2, start, sol, kry, hess):
    m = r.shape[0]
    zero = jnp.zeros((1, m), F32)
    matrix = [[zero] * ITERS for _ in range(ITERS + 1)]
    norm = norm_of(s0[...])
    for j, s in enumerate((s0, s1, s2)):
        h, length = scalars(j, s[...], norm)
        for i in range(j + 1):
            matrix[i][j] = h[i]
        matrix[j + 1][j] = length
    for i in range(ITERS + 1):
        hess[i] = jnp.concatenate(matrix[i], axis=0)
    last = matrix[3][2]
    rows = [1.0 / norm, matrix[0][2] / last / norm, matrix[1][2] / last, matrix[2][2] / last]
    rows.append(1.0 / last)
    y = least_squares(matrix, norm)
    rows += [y[0] / norm, y[1], y[2]]
    c = rows_to_columns(jnp.concatenate(rows, axis=0), 8)
    step = 128
    for k in range(r.shape[1] // step):
        s = slice(k * step, (k + 1) * step)
        a, u, v = r[:, s], k1[:, s], k2[:, s]
        kry[0, :, s] = a * c[0]
        kry[1, :, s] = u
        kry[2, :, s] = v
        kry[3, :, s] = w[:, s] * c[4] - c[1] * a - c[2] * u - c[3] * v
        sol[:, s] = start[:, s] + c[5] * p0[:, s] + c[6] * p1[:, s] + c[7] * p2[:, s]


def call(body, outs, args, scratch=(), name=None, flops=0):
    vm = pl.BlockSpec(memory_space=pltpu.VMEM)
    size = sum(a.size * a.dtype.itemsize for a in args)
    return pl.pallas_call(
        body,
        name=name,
        out_shape=[jax.ShapeDtypeStruct(s, d) for s, d in outs],
        in_specs=[vm] * len(args),
        out_specs=[vm] * len(outs),
        scratch_shapes=list(scratch),
        cost_estimate=pl.CostEstimate(flops=flops, bytes_accessed=size, transcendentals=0),
    )(*args)


def passed(value, steps):
    count = lax.axis_size("rows")
    first, last = (max(0, -steps), min(count, count - steps))
    return lax.ppermute(value, "rows", [(s, s + steps) for s in range(first, last)])


def local(bl, bd, bu, fl, pi, rhs, start):
    n, b = bd.shape[0], bd.shape[1]
    m, width = rhs.shape
    vec, edge, sq = ((m, width), F32), ((m, b), F32), ((b, b), F32)
    pads = [pltpu.VMEM((m, (n + 2) * b), BF16)] * 2
    before, after = passed(start[:, width - b :], 1), passed(start[:, :b], -1)
    g1, g2, g3 = ((n, b, 2 * b), BF16), ((n, 2 * b, 2 * b), BF16), ((n, 3 * b, 2 * b), BF16)
    gl, ge, gp, ga, gvw, wt, vb = call(
        setup_kernel, [g1, g1, g1, g3, g2, sq, sq], [bl, bd, bu, fl, pi],
        [pltpu.VMEM((n, b, b), F32)], "setup", 2 * n * 8 * 4 * b**3,
    )
    vbp = passed(vb, 1)
    wtn = passed(wt, -1)
    r, g = call(
        first_kernel, [vec, vec], [rhs, start, before, after, ga, gl, ge, gp], pads, "first",
        2 * n * 6 * 4 * b * b * m,
    )
    gbp, gtn = passed(g[:, width - b :], 1), passed(g[:, :b], -1)
    (sinv,) = call(inverse_kernel, [sq], [wt, vbp], [pltpu.VMEM((b, b), F32)], "inverse", 10**8)
    sinvn = passed(sinv, -1)
    ks, ps, sums = [r], [], []
    for j in range(ITERS):
        (p,) = call(
            pre_kernel, [vec], [g, gbp, gtn, wt, vbp, sinv, wtn, sinvn, gvw], (), f"pre{j}",
            2 * n * 2 * 4 * b * b * m,
        )
        ps.append(p)
        before, after = passed(p[:, width - b :], 1), passed(p[:, :b], -1)
        w, prods = call(
            lambda *a, j=j: mapped_kernel(j, *a), [vec, ((8, m), F32)],
            [p, before, after, ga] + ks, pads, f"mapped{j}", 2 * n * 3 * 4 * b * b * m,
        )
        sums.append(lax.psum(prods, "rows"))
        if j < ITERS - 1:
            v, g = call(
                lambda *a, j=j: orth_kernel(j, *a), [vec, vec],
                [sums[0], sums[j], w] + ks + [gl, ge, gp], (), f"orth{j}", 2 * n * 3 * 4 * b * b * m,
            )
            ks.append(v)
            gbp, gtn = passed(g[:, width - b :], 1), passed(g[:, :b], -1)
    return call(
        final_kernel, [vec, ((ITERS + 1, m, width), F32), ((ITERS + 1, ITERS, m), F32)],
        sums + ks + [w] + ps + [start], (), "final", 10**7,
    )


def solution(mesh):
    def run(*args):
        return tuple(local(*args))

    return jax.shard_map(
        run,
        mesh=mesh,
        in_specs=(P("rows", None, None),) * 5 + (P(None, "rows"),) * 2,
        out_specs=(P(None, "rows"), P(None, None, "rows"), P()),
        check_vma=False,
    )
```

time: 524 us -> 285 us (0.54); the launches traced: 515 us -> 284 us
  matrix products: 142 us -> 0 us
  local copies, waits for them, and re-layouts: 97.1 us -> 12.5 us
  Pallas kernels: 0 us -> 70.6 us
  other arithmetic: 53.4 us -> 0 us
  blocking collectives: 171 us -> 144 us
  starting transfers between devices: 40.6 us -> 50.8 us
    dot_general x307 -> x0, matrix products: 138 us -> none  [the longest x299 123 us: block_apply(): jnp.einsum('...ij,c...j->c...i', matrices, vectors, precision=highest)]
    unnamed x219 -> x34, local copies, waits for them, and re-layouts: 75.9 us -> 5.01 us
    pallas_call x0 -> x12, Pallas kernels: none -> 70.6 us  [call(): pl.pallas_call(body, name=name, out_shape=[jax.ShapeDtypeStruct(s, d) for...]
    another operation x14 -> x0, other arithmetic: 39.9 us -> none  [the longest x3 14.7 us: invert_coupling(): factor = jnp.linalg.cholesky(normal_matrix)]
    psum x4 -> x3, blocking collectives: 171 us -> 144 us  [local(): sums.append(lax.psum(prods, 'rows'))]
    another operation x12 -> x0, local copies, waits for them, and re-layouts: 16 us -> none  [the longest x8 8.29 us: local_solve(): return jnp.stack(backward[::-1], axis=-2)]
    ppermute x17, starting transfers between devices: 40.6 us -> 50.8 us  [passed(): lax.ppermute(value, 'rows', [(s, s + steps) for s in range(first, last)])]
    div x6 -> x0, other arithmetic: 6.37 us -> none  [the longest x3 3.43 us: local(): krylov.append(update / length_now[:, None, None])]
  transfers between devices with their start and end apart: 17 -> 17, of which waited for: 5 -> 6; matrix products, arithmetic and copies ran while one was open for 46% -> 1% of each run, Pallas kernels for 0% -> 4%
where the time goes in v1:
time: 285 us; the launch traced here: 284 us
  blocking collectives  144 us (51%)
  Pallas kernels  70.6 us (25%)
  starting transfers between devices  50.8 us (18%)
  local copies, waits for them, and re-layouts  12.5 us (4%)
  waiting for transfers between devices  4.97 us (2%)
    psum x3, blocking collectives, local(): sums.append(lax.psum(prods, 'rows'))  144 us
    pallas_call x12, Pallas kernels, call(): pl.pallas_call(body, name=name, out_shape=[jax.ShapeDtypeStruct(s, d) for...  70.6 us
    ppermute x17, starting transfers between devices, passed(): lax.ppermute(value, 'rows', [(s, s + steps) for s in range(first, last)])  50.8 us
  transfers between devices with their start and end apart: 17, of which 6 were waited for; matrix products, arithmetic and copies ran while one was open for 1% of the time, Pallas kernels for 4%

profile of v1, /device:TPU:0, one launch (start us, length us, event | category | flops | bytes accessed | tf_op | source)
XLA Modules:
  0.0 284.1 jit_solution(3209683646350832655)
XLA Ops:
  0.6 9.3 %setup.1 = (bf16[16,128,256]{2,1,0:T(8,128)(2,1)}, bf16[16,128,256]{2,1,0:T(8,128)(2,1)}, bf16[16,128,256]{2,1,0:T(8,128)(2,1)}, bf16[16,384,256]{2,1,0:T(8,128)...) custom-call(f32[16,128,128]{2,1,0:T(8,128)} %bl.1, f32[16,128,128]{2,1,0:T(8,128)} %bd.1, ...), custom_call_target="tpu_custom_call" | custom-call | flops 2147483648 | bytes 5242880 | tf_op jit(solution)/shard_map/setup/pallas_call | solution.py:261
  10.0 2.4 collective-permute-start.4
  14.6 5.1 %collective-permute-start = (f32[128,128]{1,0:T(8,128)S(1)}, f32[128,128]{1,0:T(8,128)S(1)}, u32[]{:S(2)}, u32[]{:S(2)}) collective-permute-start(f32[128,128]{1,0:T(8,128)S(1)} %get-tuple-element.57), channel_id=1, source_target_pairs={{0,1},{1,2},{2,3},{3,4},{4,5},{5,6},{6,7},{7,8},{8,9},{9,10},{10,1... | collective-permute-start | bytes 196616 | tf_op jit(solution)/shard_map/ppermute | solution.py:275
  19.7 1.3 collective-permute-start.5
  21.6 2.3 inverse.1.sinv
  25.9 9.2 %first.1 = (f32[128,2048]{1,0:T(8,128)}, f32[128,2048]{1,0:T(8,128)}) custom-call(f32[128,2048]{1,0:T(8,128)} %rhs.1, f32[128,2048]{1,0:T(8,128)} %start.3, f32[128,128]{1,0:T(8,128)} %copy-done.4, f32[128,128]{1,0:T(8,128)} %copy-done.3, bf16[16,384,256]{2,1,0:T(8,128)(2,1)} %get-tuple-element.22.ga.a_3_, ...), custom_call_target="tpu_custom_call" | custom-call | flops 1610612736 | bytes 8519680 | tf_op jit(solution)/shard_map/first/pallas_call | solution.py:261
  37.2 11.0 %collective-permute-start.2 = (f32[128,128]{1,0:T(8,128)S(1)}, f32[128,128]{1,0:T(8,128)S(1)}, u32[]{:S(2)}, u32[]{:S(2)}) collective-permute-start(f32[128,128]{1,0:T(8,128)S(1)} %get-tuple-element.55), channel_id=1, source_target_pairs={{0,1},{1,2},{2,3},{3,4},{4,5},{5,6},{6,7},{7,8},{8,9},{9,10},{10,1... | collective-permute-start | bytes 196616 | tf_op jit(solution)/shard_map/ppermute | solution.py:275
  49.7 4.2 %pre0.1.a_0_.p0 = f32[128,2048]{1,0:T(8,128)} custom-call(f32[128,2048]{1,0:T(8,128)} %get-tuple-element.26.g, f32[128,128]{1,0:T(8,128)} %copy-done.7, f32[128,128]{1,0:T(8,128)} %copy-done.5, f32[128,128]{1,0:T(8,128)} %get-tuple-element.27.wt, f32[128,128]{1,0:T(8,128)} %copy-done, f32[128,128]{1,0:T(8,128)} %inverse.1.sinv, f32[128,128]{1,0:T(8,128)} %copy-done.1, ...), custom_call_target="tpu_custom_call" | custom-call | flops 536870912 | bytes 3604480 | tf_op jit(solution)/shard_map/pre0/pallas_call | solution.py:261
  56.1 4.7 %collective-permute-start.7 = (f32[128,128]{1,0:T(8,128)S(1)}, f32[128,128]{1,0:T(8,128)S(1)}, u32[]{:S(2)}, u32[]{:S(2)}) collective-permute-start(f32[128,128]{1,0:T(8,128)S(1)} %get-tuple-element.53), channel_id=1, source_target_pairs={{0,1},{1,2},{2,3},{3,4},{4,5},{5,6},{6,7},{7,8},{8,9},{9,10},{10,1... | collective-permute-start | bytes 196616 | tf_op jit(solution)/shard_map/ppermute | solution.py:275
  62.4 4.6 %mapped0.1 = (f32[128,2048]{1,0:T(8,128)}, f32[8,128]{1,0:T(8,128)}) custom-call(f32[128,2048]{1,0:T(8,128)} %pre0.1.a_0_.p0, f32[128,128]{1,0:T(8,128)} %copy-done.14, f32[128,128]{1,0:T(8,128)} %copy-done.9, bf16[16,384,256]{2,1,0:T(8,128)(2,1)} %get-tuple-element.22.ga.a_3_, f32[128,2048]{1,0:T(8,128)} %get-tuple-element.30.a_4_.a_3_.r), custom_call_target="tpu_custom_call" | custom-call | flops 805306368 | bytes 5373952 | tf_op jit(solution)/shard_map/mapped0/pallas_call | solution.py:261
  67.0 50.5 %psum.21.a_0_.a_1_.s0 = f32[8,128]{1,0:T(8,128)} all-reduce(f32[8,128]{1,0:T(8,128)} %get-tuple-element.31), channel_id=1, replica_groups=mesh['rows'=32] {'rows'}, use_global_device_ids=true, to_apply=%region_0.0 | all-reduce | flops 1024 | bytes 8192 | tf_op jit(solution)/shard_map/psum | solution.py:310
  117.5 7.6 %orth0.1 = (f32[128,2048]{1,0:T(8,128)}, f32[128,2048]{1,0:T(8,128)}) custom-call(f32[8,128]{1,0:T(8,128)} %psum.21.a_0_.a_1_.s0, f32[8,128]{1,0:T(8,128)} %psum.21.a_0_.a_1_.s0, f32[128,2048]{1,0:T(8,128)} %get-tuple-element.32.a_2_, f32[128,2048]{1,0:T(8,128)} %get-tuple-element.30.a_4_.a_3_.r, bf16[16,128,256]{2,1,0:T(8,128)(2,1)} %get-tuple-element.23.gl.a_4_.a_5_, ...), custom_call_target="tpu_custom_call" | custom-call | flops 805306368 | bytes 5251072 | tf_op jit(solution)/shard_map/orth0/pallas_call | solution.py:261
  127.3 3.2 %collective-permute-start.9 = (f32[128,128]{1,0:T(8,128)S(1)}, f32[128,128]{1,0:T(8,128)S(1)}, u32[]{:S(2)}, u32[]{:S(2)}) collective-permute-start(f32[128,128]{1,0:T(8,128)S(1)} %get-tuple-element.51), channel_id=1, source_target_pairs={{0,1},{1,2},{2,3},{3,4},{4,5},{5,6},{6,7},{7,8},{8,9},{9,10},{10,1... | collective-permute-start | bytes 196616 | tf_op jit(solution)/shard_map/ppermute | solution.py:275
  131.8 4.3 %pre1.1.a_0_.p1 = f32[128,2048]{1,0:T(8,128)} custom-call(f32[128,2048]{1,0:T(8,128)} %get-tuple-element.33.g, f32[128,128]{1,0:T(8,128)} %copy-done.16, f32[128,128]{1,0:T(8,128)} %copy-done.12, f32[128,128]{1,0:T(8,128)} %get-tuple-element.27.wt, f32[128,128]{1,0:T(8,128)} %copy-done, f32[128,128]{1,0:T(8,128)} %inverse.1.sinv, f32[128,128]{1,0:T(8,128)} %copy-done.1, ...), custom_call_target="tpu_custom_call" | custom-call | flops 536870912 | bytes 3604480 | tf_op jit(solution)/shard_map/pre1/pallas_call | solution.py:261
  138.3 4.9 %collective-permute-start.11 = (f32[128,128]{1,0:T(8,128)S(1)}, f32[128,128]{1,0:T(8,128)S(1)}, u32[]{:S(2)}, u32[]{:S(2)}) collective-permute-start(f32[128,128]{1,0:T(8,128)S(1)} %get-tuple-element.49), channel_id=1, source_target_pairs={{0,1},{1,2},{2,3},{3,4},{4,5},{5,6},{6,7},{7,8},{8,9},{9,10},{10,1... | collective-permute-start | bytes 196616 | tf_op jit(solution)/shard_map/ppermute | solution.py:275
  144.7 4.9 %mapped1.1 = (f32[128,2048]{1,0:T(8,128)}, f32[8,128]{1,0:T(8,128)}) custom-call(f32[128,2048]{1,0:T(8,128)} %pre1.1.a_0_.p1, f32[128,128]{1,0:T(8,128)} %copy-done.15, f32[128,128]{1,0:T(8,128)} %copy-done.10, bf16[16,384,256]{2,1,0:T(8,128)(2,1)} %get-tuple-element.22.ga.a_3_, f32[128,2048]{1,0:T(8,128)} %get-tuple-element.30.a_4_.a_3_.r, ...), custom_call_target="tpu_custom_call" | custom-call | flops 805306368 | bytes 6422528 | tf_op jit(solution)/shard_map/mapped1/pallas_call | solution.py:261
  149.6 47.0 %psum.22.a_1_.s1 = f32[8,128]{1,0:T(8,128)} all-reduce(f32[8,128]{1,0:T(8,128)} %get-tuple-element.35), channel_id=1, replica_groups=mesh['rows'=32] {'rows'}, use_global_device_ids=true, to_apply=%region_1.0 | all-reduce | flops 1024 | bytes 8192 | tf_op jit(solution)/shard_map/psum | solution.py:310
  196.6 7.9 %orth1.1 = (f32[128,2048]{1,0:T(8,128)}, f32[128,2048]{1,0:T(8,128)}) custom-call(f32[8,128]{1,0:T(8,128)} %psum.21.a_0_.a_1_.s0, f32[8,128]{1,0:T(8,128)} %psum.22.a_1_.s1, f32[128,2048]{1,0:T(8,128)} %get-tuple-element.36.a_2_, f32[128,2048]{1,0:T(8,128)} %get-tuple-element.30.a_4_.a_3_.r, f32[128,2048]{1,0:T(8,128)} %get-tuple-element.34.a_5_.a_4_.k1, ...), custom_call_target="tpu_custom_call" | custom-call | flops 805306368 | bytes 6299648 | tf_op jit(solution)/shard_map/orth1/pallas_call | solution.py:261
  206.7 3.0 %collective-permute-start.13 = (f32[128,128]{1,0:T(8,128)S(1)}, f32[128,128]{1,0:T(8,128)S(1)}, u32[]{:S(2)}, u32[]{:S(2)}) collective-permute-start(f32[128,128]{1,0:T(8,128)S(1)} %get-tuple-element.47), channel_id=1, source_target_pairs={{0,1},{1,2},{2,3},{3,4},{4,5},{5,6},{6,7},{7,8},{8,9},{9,10},{10,1... | collective-permute-start | bytes 196616 | tf_op jit(solution)/shard_map/ppermute | solution.py:275
  211.2 4.2 %pre2.1.a_0_.p2 = f32[128,2048]{1,0:T(8,128)} custom-call(f32[128,2048]{1,0:T(8,128)} %get-tuple-element.37.g, f32[128,128]{1,0:T(8,128)} %copy-done.11, f32[128,128]{1,0:T(8,128)} %copy-done.6, f32[128,128]{1,0:T(8,128)} %get-tuple-element.27.wt, f32[128,128]{1,0:T(8,128)} %copy-done, f32[128,128]{1,0:T(8,128)} %inverse.1.sinv, f32[128,128]{1,0:T(8,128)} %copy-done.1, ...), custom_call_target="tpu_custom_call" | custom-call | flops 536870912 | bytes 3604480 | tf_op jit(solution)/shard_map/pre2/pallas_call | solution.py:261
  217.6 4.9 %collective-permute-start.15 = (f32[128,128]{1,0:T(8,128)S(1)}, f32[128,128]{1,0:T(8,128)S(1)}, u32[]{:S(2)}, u32[]{:S(2)}) collective-permute-start(f32[128,128]{1,0:T(8,128)S(1)} %get-tuple-element.45), channel_id=1, source_target_pairs={{0,1},{1,2},{2,3},{3,4},{4,5},{5,6},{6,7},{7,8},{8,9},{9,10},{10,1... | collective-permute-start | bytes 196616 | tf_op jit(solution)/shard_map/ppermute | solution.py:275
  224.0 5.3 %mapped2.1 = (f32[128,2048]{1,0:T(8,128)}, f32[8,128]{1,0:T(8,128)}) custom-call(f32[128,2048]{1,0:T(8,128)} %pre2.1.a_0_.p2, f32[128,128]{1,0:T(8,128)} %copy-done.13, f32[128,128]{1,0:T(8,128)} %copy-done.8, bf16[16,384,256]{2,1,0:T(8,128)(2,1)} %get-tuple-element.22.ga.a_3_, f32[128,2048]{1,0:T(8,128)} %get-tuple-element.30.a_4_.a_3_.r, ...), custom_call_target="tpu_custom_call" | custom-call | flops 805306368 | bytes 7471104 | tf_op jit(solution)/shard_map/mapped2/pallas_call | solution.py:261
  229.3 46.9 %psum.23.s2 = f32[8,128]{1,0:T(8,128)} all-reduce(f32[8,128]{1,0:T(8,128)} %get-tuple-element.39), channel_id=1, replica_groups=mesh['rows'=32] {'rows'}, use_global_device_ids=true, to_apply=%region_2.0 | all-reduce | flops 1024 | bytes 8192 | tf_op jit(solution)/shard_map/psum | solution.py:310
  276.2 6.7 %final.1 = (f32[128,2048]{1,0:T(8,128)}, f32[4,128,2048]{2,1,0:T(8,128)}, f32[4,3,128]{2,1,0:T(4,128)}) custom-call(f32[8,128]{1,0:T(8,128)} %psum.21.a_0_.a_1_.s0, f32[8,128]{1,0:T(8,128)} %psum.22.a_1_.s1, f32[8,128]{1,0:T(8,128)} %psum.23.s2, f32[128,2048]{1,0:T(8,128)} %get-tuple-element.30.a_4_.a_3_.r, f32[128,2048]{1,0:T(8,128)} %get-tuple-element.34.a_5_.a_4_.k1, ...), custom_call_target="tpu_custom_call" | custom-call | flops 10000000 | bytes 8400896 | tf_op jit(solution)/shard_map/final/pallas_call | solution.py:261
  (67 shorter events, 27.8 us)
Async XLA Ops:
  10.0 11.0 %collective-permute-start.4 = (f32[128,128]{1,0:T(8,128)}, f32[128,128]{1,0:T(8,128)S(1)}, u32[]{:S(2)}, u32[]{:S(2)}) collective-permute-start(f32[128,128]{1,0:T(8,128)} %get-tuple-element.28), channel_id=1, source_target_pairs={{0,1},{1,2},{2,3},{3,4},{4,5},{5,6},{6,7},{7,8},{8,9},{9,10},{10,1... | collective-permute-start | bytes 196616 | tf_op jit(solution)/shard_map/ppermute | solution.py:275
  13.3 11.9 %collective-permute-start.1 = (f32[128,128]{1,0:T(8,128)S(1)}, f32[128,128]{1,0:T(8,128)S(1)}, u32[]{:S(2)}, u32[]{:S(2)}) collective-permute-start(f32[128,128]{1,0:T(8,128)S(1)} %get-tuple-element.56), channel_id=1, source_target_pairs={{1,0},{2,1},{3,2},{4,3},{5,4},{6,5},{7,6},{8,7},{9,8},{10,9},{11,1... | collective-permute-start | bytes 196616 | tf_op jit(solution)/shard_map/ppermute | solution.py:275
  14.6 10.7 %collective-permute-start = (f32[128,128]{1,0:T(8,128)S(1)}, f32[128,128]{1,0:T(8,128)S(1)}, u32[]{:S(2)}, u32[]{:S(2)}) collective-permute-start(f32[128,128]{1,0:T(8,128)S(1)} %get-tuple-element.57), channel_id=1, source_target_pairs={{0,1},{1,2},{2,3},{3,4},{4,5},{5,6},{6,7},{7,8},{8,9},{9,10},{10,1... | collective-permute-start | bytes 196616 | tf_op jit(solution)/shard_map/ppermute | solution.py:275
  19.7 28.5 %collective-permute-start.5 = (f32[128,128]{1,0:T(8,128)}, f32[128,128]{1,0:T(8,128)S(1)}, u32[]{:S(2)}, u32[]{:S(2)}) collective-permute-start(f32[128,128]{1,0:T(8,128)} %get-tuple-element.27.wt), channel_id=1, source_target_pairs={{1,0},{2,1},{3,2},{4,3},{5,4},{6,5},{7,6},{8,7},{9,8},{10,9},{11,1... | collective-permute-start | bytes 196616 | tf_op jit(solution)/shard_map/ppermute | solution.py:275
  23.9 24.3 %collective-permute-start.6 = (f32[128,128]{1,0:T(8,128)}, f32[128,128]{1,0:T(8,128)S(1)}, u32[]{:S(2)}, u32[]{:S(2)}) collective-permute-start(f32[128,128]{1,0:T(8,128)} %inverse.1.sinv), channel_id=1, source_target_pairs={{1,0},{2,1},{3,2},{4,3},{5,4},{6,5},{7,6},{8,7},{9,8},{10,9},{11,1... | collective-permute-start | bytes 196616 | tf_op jit(solution)/shard_map/ppermute | solution.py:275
  35.9 12.3 %collective-permute-start.3 = (f32[128,128]{1,0:T(8,128)S(1)}, f32[128,128]{1,0:T(8,128)S(1)}, u32[]{:S(2)}, u32[]{:S(2)}) collective-permute-start(f32[128,128]{1,0:T(8,128)S(1)} %get-tuple-element.54), channel_id=1, source_target_pairs={{1,0},{2,1},{3,2},{4,3},{5,4},{6,5},{7,6},{8,7},{9,8},{10,9},{11,1... | collective-permute-start | bytes 196616 | tf_op jit(solution)/shard_map/ppermute | solution.py:275
  37.2 11.8 %collective-permute-start.2 = (f32[128,128]{1,0:T(8,128)S(1)}, f32[128,128]{1,0:T(8,128)S(1)}, u32[]{:S(2)}, u32[]{:S(2)}) collective-permute-start(f32[128,128]{1,0:T(8,128)S(1)} %get-tuple-element.55), channel_id=1, source_target_pairs={{0,1},{1,2},{2,3},{3,4},{4,5},{5,6},{6,7},{7,8},{8,9},{9,10},{10,1... | collective-permute-start | bytes 196616 | tf_op jit(solution)/shard_map/ppermute | solution.py:275
  48.2 0.9 copy-start.1
  48.2 0.9 copy-start.2
  48.2 0.8 copy-start.5
  54.8 6.0 %collective-permute-start.8 = (f32[128,128]{1,0:T(8,128)S(1)}, f32[128,128]{1,0:T(8,128)S(1)}, u32[]{:S(2)}, u32[]{:S(2)}) collective-permute-start(f32[128,128]{1,0:T(8,128)S(1)} %get-tuple-element.52), channel_id=1, source_target_pairs={{1,0},{2,1},{3,2},{4,3},{5,4},{6,5},{7,6},{8,7},{9,8},{10,9},{11,1... | collective-permute-start | bytes 196616 | tf_op jit(solution)/shard_map/ppermute | solution.py:275
  56.1 5.6 %collective-permute-start.7 = (f32[128,128]{1,0:T(8,128)S(1)}, f32[128,128]{1,0:T(8,128)S(1)}, u32[]{:S(2)}, u32[]{:S(2)}) collective-permute-start(f32[128,128]{1,0:T(8,128)S(1)} %get-tuple-element.53), channel_id=1, source_target_pairs={{0,1},{1,2},{2,3},{3,4},{4,5},{5,6},{6,7},{7,8},{8,9},{9,10},{10,1... | collective-permute-start | bytes 196616 | tf_op jit(solution)/shard_map/ppermute | solution.py:275
  60.9 0.9 copy-start.9
  126.0 4.5 %collective-permute-start.10 = (f32[128,128]{1,0:T(8,128)S(1)}, f32[128,128]{1,0:T(8,128)S(1)}, u32[]{:S(2)}, u32[]{:S(2)}) collective-permute-start(f32[128,128]{1,0:T(8,128)S(1)} %get-tuple-element.50), channel_id=1, source_target_pairs={{1,0},{2,1},{3,2},{4,3},{5,4},{6,5},{7,6},{8,7},{9,8},{10,9},{11,1... | collective-permute-start | bytes 196616 | tf_op jit(solution)/shard_map/ppermute | solution.py:275
  127.3 3.9 %collective-permute-start.9 = (f32[128,128]{1,0:T(8,128)S(1)}, f32[128,128]{1,0:T(8,128)S(1)}, u32[]{:S(2)}, u32[]{:S(2)}) collective-permute-start(f32[128,128]{1,0:T(8,128)S(1)} %get-tuple-element.51), channel_id=1, source_target_pairs={{0,1},{1,2},{2,3},{3,4},{4,5},{5,6},{6,7},{7,8},{8,9},{9,10},{10,1... | collective-permute-start | bytes 196616 | tf_op jit(solution)/shard_map/ppermute | solution.py:275
  137.0 6.2 %collective-permute-start.12 = (f32[128,128]{1,0:T(8,128)S(1)}, f32[128,128]{1,0:T(8,128)S(1)}, u32[]{:S(2)}, u32[]{:S(2)}) collective-permute-start(f32[128,128]{1,0:T(8,128)S(1)} %get-tuple-element.48), channel_id=1, source_target_pairs={{1,0},{2,1},{3,2},{4,3},{5,4},{6,5},{7,6},{8,7},{9,8},{10,9},{11,1... | collective-permute-start | bytes 196616 | tf_op jit(solution)/shard_map/ppermute | solution.py:275
  138.3 5.7 %collective-permute-start.11 = (f32[128,128]{1,0:T(8,128)S(1)}, f32[128,128]{1,0:T(8,128)S(1)}, u32[]{:S(2)}, u32[]{:S(2)}) collective-permute-start(f32[128,128]{1,0:T(8,128)S(1)} %get-tuple-element.49), channel_id=1, source_target_pairs={{0,1},{1,2},{2,3},{3,4},{4,5},{5,6},{6,7},{7,8},{8,9},{9,10},{10,1... | collective-permute-start | bytes 196616 | tf_op jit(solution)/shard_map/ppermute | solution.py:275
  143.2 0.9 copy-start.10
  205.4 4.3 %collective-permute-start.14 = (f32[128,128]{1,0:T(8,128)S(1)}, f32[128,128]{1,0:T(8,128)S(1)}, u32[]{:S(2)}, u32[]{:S(2)}) collective-permute-start(f32[128,128]{1,0:T(8,128)S(1)} %get-tuple-element.46), channel_id=1, source_target_pairs={{1,0},{2,1},{3,2},{4,3},{5,4},{6,5},{7,6},{8,7},{9,8},{10,9},{11,1... | collective-permute-start | bytes 196616 | tf_op jit(solution)/shard_map/ppermute | solution.py:275
  206.7 3.9 %collective-permute-start.13 = (f32[128,128]{1,0:T(8,128)S(1)}, f32[128,128]{1,0:T(8,128)S(1)}, u32[]{:S(2)}, u32[]{:S(2)}) collective-permute-start(f32[128,128]{1,0:T(8,128)S(1)} %get-tuple-element.47), channel_id=1, source_target_pairs={{0,1},{1,2},{2,3},{3,4},{4,5},{5,6},{6,7},{7,8},{8,9},{9,10},{10,1... | collective-permute-start | bytes 196616 | tf_op jit(solution)/shard_map/ppermute | solution.py:275
  209.7 0.9 copy-start.6
  216.3 6.2 %collective-permute-start.16 = (f32[128,128]{1,0:T(8,128)S(1)}, f32[128,128]{1,0:T(8,128)S(1)}, u32[]{:S(2)}, u32[]{:S(2)}) collective-permute-start(f32[128,128]{1,0:T(8,128)S(1)} %get-tuple-element.44), channel_id=1, source_target_pairs={{1,0},{2,1},{3,2},{4,3},{5,4},{6,5},{7,6},{8,7},{9,8},{10,9},{11,1... | collective-permute-start | bytes 196616 | tf_op jit(solution)/shard_map/ppermute | solution.py:275
  217.6 5.7 %collective-permute-start.15 = (f32[128,128]{1,0:T(8,128)S(1)}, f32[128,128]{1,0:T(8,128)S(1)}, u32[]{:S(2)}, u32[]{:S(2)}) collective-permute-start(f32[128,128]{1,0:T(8,128)S(1)} %get-tuple-element.45), channel_id=1, source_target_pairs={{0,1},{1,2},{2,3},{3,4},{4,5},{5,6},{6,7},{7,8},{8,9},{9,10},{10,1... | collective-permute-start | bytes 196616 | tf_op jit(solution)/shard_map/ppermute | solution.py:275
  222.5 0.9 copy-start.8
  (10 other events, 6.3 us)

commit v2 on v1

--- a/solution.py
+++ b/solution.py
@@ -269,10 +269,126 @@
     )(*args)
 
 
-def passed(value, steps):
+def exchange_kernel(up, down, before, after, send, recv):
+    me, count = lax.axis_index("rows"), lax.axis_size("rows")
+    b = before.shape[1]
+    barrier = pltpu.get_barrier_semaphore()
+    inner, outer = me > 0, me < count - 1
+
+    def copy(src, dst, i, device):
+        return pltpu.make_async_remote_copy(
+            src_ref=src, dst_ref=dst, send_sem=send.at[i], recv_sem=recv.at[i],
+            device_id=(device,), device_id_type=pl.DeviceIdType.MESH,
+        )
+
+    to_next = lambda: copy(up.at[:, up.shape[1] - b :], before, 0, me + 1)
+    to_prev = lambda: copy(down.at[:, 0:b], after, 1, me - 1)
+
+    @pl.when(inner)
+    def _():
+        pl.semaphore_signal(barrier, 1, device_id=(me - 1,), device_id_type=pl.DeviceIdType.MESH)
+
+    @pl.when(outer)
+    def _():
+        pl.semaphore_signal(barrier, 1, device_id=(me + 1,), device_id_type=pl.DeviceIdType.MESH)
+
+    @pl.when(inner & outer)
+    def _():
+        pl.semaphore_wait(barrier, 2)
+
+    @pl.when(~(inner & outer))
+    def _():
+        pl.semaphore_wait(barrier, 1)
+
+    @pl.when(outer)
+    def _():
+        to_next().start()
+
+    @pl.when(inner)
+    def _():
+        to_prev().start()
+
+    @pl.when(me == 0)
+    def _():
+        before[...] = jnp.zeros_like(before)
+
+    @pl.when(me == count - 1)
+    def _():
+        after[...] = jnp.zeros_like(after)
+
+    @pl.when(outer)
+    def _():
+        to_next().wait_send()
+        copy(down.at[:, 0:b], after, 1, me + 1).wait_recv()
+
+    @pl.when(inner)
+    def _():
+        to_prev().wait_send()
+        copy(up.at[:, up.shape[1] - b :], before, 0, me - 1).wait_recv()
+
+
+def exchange(up, down, b, number):
+    shape = jax.ShapeDtypeStruct((up.shape[0], b), F32)
+    return pl.pallas_call(
+        exchange_kernel,
+        name="exchange",
+        out_shape=[shape, shape],
+        in_specs=[pl.BlockSpec(memory_space=pl.ANY)] * 2,
+        out_specs=[pl.BlockSpec(memory_space=pltpu.VMEM)] * 2,
+        scratch_shapes=[pltpu.SemaphoreType.DMA((2,))] * 2,
+        compiler_params=pltpu.CompilerParams(collective_id=number, has_side_effects=True),
+    )(up, down)
+
+
+def reduce_kernel(x, out, slots, send, recv):
+    me, count = lax.axis_index("rows"), lax.axis_size("rows")
+    barrier = pltpu.get_barrier_semaphore()
+
+    def copy(k, slot, device):
+        return pltpu.make_async_remote_copy(
+            src_ref=x, dst_ref=slots.at[slot], send_sem=send.at[k], recv_sem=recv.at[slot],
+            device_id=(device,), device_id_type=pl.DeviceIdType.MESH,
+        )
+
+    @pl.loop(1, count)
+    def _(k):
+        pl.semaphore_signal(
+            barrier, 1, device_id=(lax.rem(me + k, count),), device_id_type=pl.DeviceIdType.MESH
+        )
+
+    pl.semaphore_wait(barrier, count - 1)
+
+    @pl.loop(1, count)
+    def _(k):
+        copy(k, me, lax.rem(me + k, count)).start()
+
+    slots[me] = x[...]
+
+    @pl.loop(1, count)
+    def _(k):
+        other = lax.rem(me + k, count)
+        copy(k, me, other).wait_send()
+        copy(k, other, other).wait_recv()
+
+    total = slots[0]
+    for i in range(1, count):
+        total = total + slots[i]
+    out[...] = total
+
+
+def all_sum(x):
     count = lax.axis_size("rows")
-    first, last = (max(0, -steps), min(count, count - steps))
-    return lax.ppermute(value, "rows", [(s, s + steps) for s in range(first, last)])
+    vm = pl.BlockSpec(memory_space=pltpu.VMEM)
+    return pl.pallas_call(
+        reduce_kernel,
+        name="allsum",
+        out_shape=jax.ShapeDtypeStruct(x.shape, F32),
+        in_specs=[vm],
+        out_specs=vm,
+        scratch_shapes=[pltpu.VMEM((count,) + x.shape, F32)]
+        + [pltpu.SemaphoreType.DMA((count,))] * 2,
+        compiler_params=pltpu.CompilerParams(collective_id=3, has_side_effects=True),
+    )(x)
 
 
 def local(bl, bd, bu, fl, pi, rhs, start):
@@ -280,21 +396,20 @@
     m, width = rhs.shape
     vec, edge, sq = ((m, width), F32), ((m, b), F32), ((b, b), F32)
     pads = [pltpu.VMEM((m, (n + 2) * b), BF16)] * 2
-    before, after = passed(start[:, width - b :], 1), passed(start[:, :b], -1)
+    before, after = exchange(start, start, b, 1)
     g1, g2, g3 = ((n, b, 2 * b), BF16), ((n, 2 * b, 2 * b), BF16), ((n, 3 * b, 2 * b), BF16)
     gl, ge, gp, ga, gvw, wt, vb = call(
         setup_kernel, [g1, g1, g1, g3, g2, sq, sq], [bl, bd, bu, fl, pi],
         [pltpu.VMEM((n, b, b), F32)], "setup", 2 * n * 8 * 4 * b**3,
     )
-    vbp = passed(vb, 1)
-    wtn = passed(wt, -1)
+    vbp, wtn = exchange(vb, wt, b, 2)
     r, g = call(
         first_kernel, [vec, vec], [rhs, start, before, after, ga, gl, ge, gp], pads, "first",
         2 * n * 6 * 4 * b * b * m,
     )
-    gbp, gtn = passed(g[:, width - b :], 1), passed(g[:, :b], -1)
+    gbp, gtn = exchange(g, g, b, 1)
     (sinv,) = call(inverse_kernel, [sq], [wt, vbp], [pltpu.VMEM((b, b), F32)], "inverse", 10**8)
-    sinvn = passed(sinv, -1)
+    _, sinvn = exchange(sinv, sinv, b, 2)
     ks, ps, sums = [r], [], []
     for j in range(ITERS):
         (p,) = call(
@@ -302,19 +417,19 @@
             2 * n * 2 * 4 * b * b * m,
         )
         ps.append(p)
-        before, after = passed(p[:, width - b :], 1), passed(p[:, :b], -1)
+        before, after = exchange(p, p, b, 1)
         w, prods = call(
             lambda *a, j=j: mapped_kernel(j, *a), [vec, ((8, m), F32)],
             [p, before, after, ga] + ks, pads, f"mapped{j}", 2 * n * 3 * 4 * b * b * m,
         )
-        sums.append(lax.psum(prods, "rows"))
+        sums.append(all_sum(prods))
         if j < ITERS - 1:
             v, g = call(
                 lambda *a, j=j: orth_kernel(j, *a), [vec, vec],
                 [sums[0], sums[j], w] + ks + [gl, ge, gp], (), f"orth{j}", 2 * n * 3 * 4 * b * b * m,
             )
             ks.append(v)
-            gbp, gtn = passed(g[:, width - b :], 1), passed(g[:, :b], -1)
+            gbp, gtn = exchange(g, g, b, 1)
     return call(
         final_kernel, [vec, ((ITERS + 1, m, width), F32), ((ITERS + 1, ITERS, m), F32)],
         sums + ks + [w] + ps + [start], (), "final", 10**7,

time: 285 us -> 168 us (0.59)
  blocking collectives: 144 us -> 0 us
  Pallas kernels: 70.6 us -> 166 us
  starting transfers between devices: 50.8 us -> 0 us
  local copies, waits for them, and re-layouts: 12.5 us -> 1.29 us
  waiting for transfers between devices: 4.97 us -> 0 us
    psum x3 -> x0, blocking collectives: 144 us -> none  [local(): sums.append(lax.psum(prods, 'rows'))]
    pallas_call x0 -> x12, Pallas kernels: none -> 95.2 us  [the longest x3 49.5 us: all_sum(): pl.pallas_call(reduce_kernel, name='allsum', out_shape=jax.ShapeDtypeStru...]
    ppermute x17 -> x0, starting transfers between devices: 50.8 us -> none  [passed(): lax.ppermute(value, 'rows', [(s, s + steps) for s in range(first, last)])]
    slice x7 -> x0, local copies, waits for them, and re-layouts: 6.17 us -> none  [the longest x3 2.64 us: local(): before, after = (passed(p[:, width - b:], 1), passed(p[:, :b], -1))]
    unnamed x34 -> x0, local copies, waits for them, and re-layouts: 5.01 us -> none
    ppermute x17 -> x0, waiting for transfers between devices: 4.97 us -> none  [passed(): lax.ppermute(value, 'rows', [(s, s + steps) for s in range(first, last)])]
  transfers between devices with their start and end apart: 17 -> 0, of which waited for: 6 -> 0; matrix products, arithmetic and copies ran while one was open for 1% -> 0% of each run, Pallas kernels for 4% -> 0%
where the time goes in v2:
time: 168 us
  Pallas kernels  166 us (99%)
    pallas_call x12, Pallas kernels, call(): pl.pallas_call(body, name=name, out_shape=[jax.ShapeDtypeStruct(s, d) for...  70.6 us
    pallas_call x3, Pallas kernels, all_sum(): pl.pallas_call(reduce_kernel, name='allsum', out_shape=jax.ShapeDtypeStru...  49.5 us
    pallas_call x9, Pallas kernels, exchange(): pl.pallas_call(exchange_kernel, name='exchange', out_shape=[shape, shape]...  45.7 us

profile of v2, /device:TPU:0, one launch (start us, length us, event | category | flops | bytes accessed | tf_op | source)
XLA Modules:
  0.0 167.9 jit_solution(7686221363795076456)
XLA Ops:
  0.6 4.8 %exchange.9 = (f32[128,128]{1,0:T(8,128)}, f32[128,128]{1,0:T(8,128)}) custom-call(f32[128,2048]{1,0:T(8,128)} %start.3, f32[128,2048]{1,0:T(8,128)} %start.3), custom_call_target="tpu_custom_call" | custom-call | tf_op jit(solution)/shard_map/exchange/pallas_call | solution.py:332
  5.4 9.3 %setup.1 = (bf16[16,128,256]{2,1,0:T(8,128)(2,1)}, bf16[16,128,256]{2,1,0:T(8,128)(2,1)}, bf16[16,128,256]{2,1,0:T(8,128)(2,1)}, bf16[16,384,256]{2,1,0:T(8,128)...) custom-call(f32[16,128,128]{2,1,0:T(8,128)} %bl.1, f32[16,128,128]{2,1,0:T(8,128)} %bd.1, ...), custom_call_target="tpu_custom_call" | custom-call | flops 2147483648 | bytes 5242880 | tf_op jit(solution)/shard_map/setup/pallas_call | solution.py:261
  14.7 4.6 %exchange.11 = (f32[128,128]{1,0:T(8,128)}, f32[128,128]{1,0:T(8,128)}) custom-call(f32[128,128]{1,0:T(8,128)} %get-tuple-element.49.up, f32[128,128]{1,0:T(8,128)} %get-tuple-element.48.down.wt), custom_call_target="tpu_custom_call" | custom-call | tf_op jit(solution)/shard_map/exchange/pallas_call | solution.py:332
  19.3 2.3 %inverse.1.up.down.sinv = f32[128,128]{1,0:T(8,128)} custom-call(f32[128,128]{1,0:T(8,128)} %get-tuple-element.48.down.wt, f32[128,128]{1,0:T(8,128)} %get-tuple-element.50.vbp), custom_call_target="tpu_custom_call" | custom-call | flops 100000000 | bytes 131072 | tf_op jit(solution)/shard_map/inverse/pallas_call | solution.py:261
  21.6 10.2 %exchange.12 = (f32[128,128]{1,0:T(8,128)}, f32[128,128]{1,0:T(8,128)}) custom-call(f32[128,128]{1,0:T(8,128)} %inverse.1.up.down.sinv, f32[128,128]{1,0:T(8,128)} %inverse.1.up.down.sinv), custom_call_target="tpu_custom_call" | custom-call | tf_op jit(solution)/shard_map/exchange/pallas_call | solution.py:332
  31.8 9.2 %first.1 = (f32[128,2048]{1,0:T(8,128)}, f32[128,2048]{1,0:T(8,128)}) custom-call(f32[128,2048]{1,0:T(8,128)} %rhs.1, f32[128,2048]{1,0:T(8,128)} %start.3, f32[128,128]{1,0:T(8,128)} %get-tuple-element.39.before, f32[128,128]{1,0:T(8,128)} %get-tuple-element.40.after, bf16[16,384,256]{2,1,0:T(8,128)(2,1)} %get-tuple-element.41.ga.a_3_, ...), custom_call_target="tpu_custom_call" | custom-call | flops 1610612736 | bytes 8519680 | tf_op jit(solution)/shard_map/first/pallas_call | solution.py:261
  41.0 5.2 %exchange.10 = (f32[128,128]{1,0:T(8,128)}, f32[128,128]{1,0:T(8,128)}) custom-call(f32[128,2048]{1,0:T(8,128)} %get-tuple-element.45.up.down.g, f32[128,2048]{1,0:T(8,128)} %get-tuple-element.45.up.down.g), custom_call_target="tpu_custom_call" | custom-call | tf_op jit(solution)/shard_map/exchange/pallas_call | solution.py:332
  46.2 4.2 %pre0.1.up.down.a_0_.p0 = f32[128,2048]{1,0:T(8,128)} custom-call(f32[128,2048]{1,0:T(8,128)} %get-tuple-element.45.up.down.g, f32[128,128]{1,0:T(8,128)} %get-tuple-element.46.gbp, f32[128,128]{1,0:T(8,128)} %get-tuple-element.47.gtn, f32[128,128]{1,0:T(8,128)} %get-tuple-element.48.down.wt, f32[128,128]{1,0:T(8,128)} %get-tuple-element.50.vbp, ...), custom_call_target="tpu_custom_call" | custom-call | flops 536870912 | bytes 3604480 | tf_op jit(solution)/shard_map/pre0/pallas_call | solution.py:261
  50.5 5.5 %exchange.13 = (f32[128,128]{1,0:T(8,128)}, f32[128,128]{1,0:T(8,128)}) custom-call(f32[128,2048]{1,0:T(8,128)} %pre0.1.up.down.a_0_.p0, f32[128,2048]{1,0:T(8,128)} %pre0.1.up.down.a_0_.p0), custom_call_target="tpu_custom_call" | custom-call | tf_op jit(solution)/shard_map/exchange/pallas_call | solution.py:332
  56.0 4.6 %mapped0.1 = (f32[128,2048]{1,0:T(8,128)}, f32[8,128]{1,0:T(8,128)}) custom-call(f32[128,2048]{1,0:T(8,128)} %pre0.1.up.down.a_0_.p0, f32[128,128]{1,0:T(8,128)} %get-tuple-element.54.a_1_, f32[128,128]{1,0:T(8,128)} %get-tuple-element.55.a_2_, bf16[16,384,256]{2,1,0:T(8,128)(2,1)} %get-tuple-element.41.ga.a_3_, f32[128,2048]{1,0:T(8,128)} %get-tuple-element.56.a_4_.a_3_.r), custom_call_target="tpu_custom_call" | custom-call | flops 805306368 | bytes 5373952 | tf_op jit(solution)/shard_map/mapped0/pallas_call | solution.py:261
  60.6 18.6 %allsum.3.a_0_.a_1_.s0 = f32[8,128]{1,0:T(8,128)} custom-call(f32[8,128]{1,0:T(8,128)} %get-tuple-element.57.x), custom_call_target="tpu_custom_call" | custom-call | tf_op jit(solution)/shard_map/allsum/pallas_call | solution.py:382
  79.2 7.7 %orth0.1 = (f32[128,2048]{1,0:T(8,128)}, f32[128,2048]{1,0:T(8,128)}) custom-call(f32[8,128]{1,0:T(8,128)} %allsum.3.a_0_.a_1_.s0, f32[8,128]{1,0:T(8,128)} %allsum.3.a_0_.a_1_.s0, f32[128,2048]{1,0:T(8,128)} %get-tuple-element.58.a_2_, f32[128,2048]{1,0:T(8,128)} %get-tuple-element.56.a_4_.a_3_.r, bf16[16,128,256]{2,1,0:T(8,128)(2,1)} %get-tuple-element.42.gl.a_4_.a_5_, ...), custom_call_target="tpu_custom_call" | custom-call | flops 805306368 | bytes 5251072 | tf_op jit(solution)/shard_map/orth0/pallas_call | solution.py:261
  86.9 3.4 %exchange.14 = (f32[128,128]{1,0:T(8,128)}, f32[128,128]{1,0:T(8,128)}) custom-call(f32[128,2048]{1,0:T(8,128)} %get-tuple-element.59.up.down.g, f32[128,2048]{1,0:T(8,128)} %get-tuple-element.59.up.down.g), custom_call_target="tpu_custom_call" | custom-call | tf_op jit(solution)/shard_map/exchange/pallas_call | solution.py:332
  90.3 4.3 %pre1.1.up.down.a_0_.p1 = f32[128,2048]{1,0:T(8,128)} custom-call(f32[128,2048]{1,0:T(8,128)} %get-tuple-element.59.up.down.g, f32[128,128]{1,0:T(8,128)} %get-tuple-element.60.gbp, f32[128,128]{1,0:T(8,128)} %get-tuple-element.61.gtn, f32[128,128]{1,0:T(8,128)} %get-tuple-element.48.down.wt, f32[128,128]{1,0:T(8,128)} %get-tuple-element.50.vbp, ...), custom_call_target="tpu_custom_call" | custom-call | flops 536870912 | bytes 3604480 | tf_op jit(solution)/shard_map/pre1/pallas_call | solution.py:261
  94.5 4.6 %exchange.15 = (f32[128,128]{1,0:T(8,128)}, f32[128,128]{1,0:T(8,128)}) custom-call(f32[128,2048]{1,0:T(8,128)} %pre1.1.up.down.a_0_.p1, f32[128,2048]{1,0:T(8,128)} %pre1.1.up.down.a_0_.p1), custom_call_target="tpu_custom_call" | custom-call | tf_op jit(solution)/shard_map/exchange/pallas_call | solution.py:332
  99.1 4.9 %mapped1.1 = (f32[128,2048]{1,0:T(8,128)}, f32[8,128]{1,0:T(8,128)}) custom-call(f32[128,2048]{1,0:T(8,128)} %pre1.1.up.down.a_0_.p1, f32[128,128]{1,0:T(8,128)} %get-tuple-element.62.a_1_, f32[128,128]{1,0:T(8,128)} %get-tuple-element.63.a_2_, bf16[16,384,256]{2,1,0:T(8,128)(2,1)} %get-tuple-element.41.ga.a_3_, f32[128,2048]{1,0:T(8,128)} %get-tuple-element.56.a_4_.a_3_.r, ...), custom_call_target="tpu_custom_call" | custom-call | flops 805306368 | bytes 6422528 | tf_op jit(solution)/shard_map/mapped1/pallas_call | solution.py:261
  104.0 15.2 %allsum.4.a_1_.s1 = f32[8,128]{1,0:T(8,128)} custom-call(f32[8,128]{1,0:T(8,128)} %get-tuple-element.65.x), custom_call_target="tpu_custom_call" | custom-call | tf_op jit(solution)/shard_map/allsum/pallas_call | solution.py:382
  119.3 7.9 %orth1.1 = (f32[128,2048]{1,0:T(8,128)}, f32[128,2048]{1,0:T(8,128)}) custom-call(f32[8,128]{1,0:T(8,128)} %allsum.3.a_0_.a_1_.s0, f32[8,128]{1,0:T(8,128)} %allsum.4.a_1_.s1, f32[128,2048]{1,0:T(8,128)} %get-tuple-element.66.a_2_, f32[128,2048]{1,0:T(8,128)} %get-tuple-element.56.a_4_.a_3_.r, f32[128,2048]{1,0:T(8,128)} %get-tuple-element.64.a_5_.a_4_.k1, ...), custom_call_target="tpu_custom_call" | custom-call | flops 805306368 | bytes 6299648 | tf_op jit(solution)/shard_map/orth1/pallas_call | solution.py:261
  127.2 2.9 %exchange.16 = (f32[128,128]{1,0:T(8,128)}, f32[128,128]{1,0:T(8,128)}) custom-call(f32[128,2048]{1,0:T(8,128)} %get-tuple-element.67.up.down.g, f32[128,2048]{1,0:T(8,128)} %get-tuple-element.67.up.down.g), custom_call_target="tpu_custom_call" | custom-call | tf_op jit(solution)/shard_map/exchange/pallas_call | solution.py:332
  130.1 4.2 %pre2.1.up.down.a_0_.p2 = f32[128,2048]{1,0:T(8,128)} custom-call(f32[128,2048]{1,0:T(8,128)} %get-tuple-element.67.up.down.g, f32[128,128]{1,0:T(8,128)} %get-tuple-element.68.gbp, f32[128,128]{1,0:T(8,128)} %get-tuple-element.69.gtn, f32[128,128]{1,0:T(8,128)} %get-tuple-element.48.down.wt, f32[128,128]{1,0:T(8,128)} %get-tuple-element.50.vbp, ...), custom_call_target="tpu_custom_call" | custom-call | flops 536870912 | bytes 3604480 | tf_op jit(solution)/shard_map/pre2/pallas_call | solution.py:261
  134.3 4.6 %exchange.17 = (f32[128,128]{1,0:T(8,128)}, f32[128,128]{1,0:T(8,128)}) custom-call(f32[128,2048]{1,0:T(8,128)} %pre2.1.up.down.a_0_.p2, f32[128,2048]{1,0:T(8,128)} %pre2.1.up.down.a_0_.p2), custom_call_target="tpu_custom_call" | custom-call | tf_op jit(solution)/shard_map/exchange/pallas_call | solution.py:332
  138.9 5.3 %mapped2.1 = (f32[128,2048]{1,0:T(8,128)}, f32[8,128]{1,0:T(8,128)}) custom-call(f32[128,2048]{1,0:T(8,128)} %pre2.1.up.down.a_0_.p2, f32[128,128]{1,0:T(8,128)} %get-tuple-element.70.a_1_, f32[128,128]{1,0:T(8,128)} %get-tuple-element.71.a_2_, bf16[16,384,256]{2,1,0:T(8,128)(2,1)} %get-tuple-element.41.ga.a_3_, f32[128,2048]{1,0:T(8,128)} %get-tuple-element.56.a_4_.a_3_.r, ...), custom_call_target="tpu_custom_call" | custom-call | flops 805306368 | bytes 7471104 | tf_op jit(solution)/shard_map/mapped2/pallas_call | solution.py:261
  144.2 15.7 %allsum.5.s2 = f32[8,128]{1,0:T(8,128)} custom-call(f32[8,128]{1,0:T(8,128)} %get-tuple-element.73.x), custom_call_target="tpu_custom_call" | custom-call | tf_op jit(solution)/shard_map/allsum/pallas_call | solution.py:382
  159.9 6.7 %final.1 = (f32[128,2048]{1,0:T(8,128)}, f32[4,128,2048]{2,1,0:T(8,128)}, f32[4,3,128]{2,1,0:T(4,128)}) custom-call(f32[8,128]{1,0:T(8,128)} %allsum.3.a_0_.a_1_.s0, f32[8,128]{1,0:T(8,128)} %allsum.4.a_1_.s1, f32[8,128]{1,0:T(8,128)} %allsum.5.s2, f32[128,2048]{1,0:T(8,128)} %get-tuple-element.56.a_4_.a_3_.r, f32[128,2048]{1,0:T(8,128)} %get-tuple-element.64.a_5_.a_4_.k1, ...), custom_call_target="tpu_custom_call" | custom-call | flops 10000000 | bytes 8400896 | tf_op jit(solution)/shard_map/final/pallas_call | solution.py:261
  (1 shorter events, 1.3 us)
